TPU v7x, 32 devices: a whole 2x2x4 slice. The times are simulated.
32 devices in a mesh: groups: 2 (over y), rows: 4 (over z), keys: 2 (over x), heads: 2 (over core).
Axes of the slice: x: 2, y: 2, z: 4, core: 2. Of those that a mesh axis runs over, the one named last changes fastest.
Arguments:
- pair: bfloat16 [1024, 512, 128], P(('groups', 'rows'), 'keys'), parts along dimension 0, may hold values from -6 to 6
- seq_length: int32 [2], P('groups'), parts along dimension 0, may hold values from 257 to 512
- tile_counts: int32 [1024, 4], P(('groups', 'rows')), parts along dimension 0, may hold values from 0 to 128, as said below
- ln_gain: float32 [128], replicated, may hold values from 0.5 to 1.5
- w_query: bfloat16 [128, 128], P(None, 'heads'), may hold values from -8 to 8
- w_key: bfloat16 [128, 128], P(None, 'heads'), may hold values from -0.5 to 0.5
- w_value: bfloat16 [128, 128], P(None, 'heads'), may hold values from -0.5 to 0.5
- w_gate: bfloat16 [128, 128], P(None, 'heads'), may hold values from -0.5 to 0.5
- w_bias: bfloat16 [128, 4], P(None, 'heads'), may hold values from -1.5 to 1.5
- w_out: bfloat16 [128, 128], replicated, may hold values from -2 to 2
Outputs:
- update: bfloat16 [1024, 512, 128], P(('groups', 'rows'), ('keys', 'heads')), parts along dimension 0
There are 2 independent parts, one for each index of `groups`. A program takes and returns all parts, laid end to end along the dimension named above; an argument that names none is the same for every part. Nothing has to cross between parts.
Inputs may be any that keep to these rules, and one draw needn't show every extreme that they name: `tile_counts`: for each row and each tile of 128 keys, how many of the tile's leading keys are valid; some rows have no valid key at all.
All inputs are finite; a program needn't handle non-finite values.
Results may differ from a plain program's by a relative error of at most 0.03.
The roundings to bfloat16 on the way count: a program that leaves them out, or rounds other values in their place, can miss the bound.
Values may be sent and summed in bfloat16 or wider, within the bound.
A program may use at most 192 MiB of HBM per device.

v0:
```python
import functools

import jax
import jax.numpy as jnp
from jax import lax
from jax.experimental import pallas as pl
from jax.experimental.pallas import tpu as pltpu
from jax.sharding import PartitionSpec as P

HEAD_DIM = 32
TILE = 128
QUERY_TILE = 512
UNROLL = 1

norm_epsilon = 1e-05
masked_score = -1e30


def layer_norm(values, gain):
    center = values - jnp.mean(values, axis=-1, keepdims=True)
    spread = jnp.mean(center * center, axis=-1, keepdims=True)
    return center * lax.rsqrt(spread + norm_epsilon) * gain


def dot_nt(a, b):
    return lax.dot_general(a, b, (((1,), (1,)), ((), ())), preferred_element_type=jnp.float32)


def bias_kernel(_, pair_ref, gain_ref, w_ref, out_ref):
    rows, cols, channels = pair_ref.shape
    flat = pair_ref[...].reshape(rows * cols, channels).astype(jnp.float32)
    normed = layer_norm(flat, gain_ref[...]).astype(jnp.bfloat16)
    out_ref[...] = dot_nt(w_ref[...], normed).astype(jnp.bfloat16)


def pair_bias_part(pair, share, rows, gain, w_bias_t):
    _, cols, channels = pair.shape
    heads_pad = w_bias_t.shape[0]
    block = min(rows, 8)
    steps = rows // block
    return pl.pallas_call(
        bias_kernel,
        grid_spec=pltpu.PrefetchScalarGridSpec(
            num_scalar_prefetch=1,
            grid=(steps,),
            in_specs=[
                pl.BlockSpec((block, cols, channels), lambda r, which: (which[0] * steps + r, 0, 0)),
                pl.BlockSpec((1, channels), lambda r, which: (0, 0)),
                pl.BlockSpec((heads_pad, channels), lambda r, which: (0, 0)),
            ],
            out_specs=pl.BlockSpec((heads_pad, block * cols), lambda r, which: (0, r)),
        ),
        out_shape=jax.ShapeDtypeStruct((heads_pad, rows * cols), jnp.bfloat16),
        cost_estimate=pl.CostEstimate(
            flops=rows * cols * channels * 40, bytes_accessed=rows * cols * channels * 2,
            transcendentals=0,
        ),
        name="pair_bias",
    )(share, pair, gain, w_bias_t)


def attention_kernel(
    seq_ref, counts_ref, pair_ref, gain_ref, w_ref, w_out_ref, bias_ref, out_ref,
    query_s, key_s, value_s, gate_s, *, row_base,
):
    parts, _, cols, channels = pair_ref.shape
    length = parts * cols
    heads = bias_ref.shape[0]
    row = row_base + pl.program_id(0)
    seq_length = seq_ref[0]

    lane = lax.broadcasted_iota(jnp.int32, (TILE, channels), 1)
    depth = lax.broadcasted_iota(jnp.int32, (TILE, channels), 0)

    @pl.when(pl.program_id(0) == 0)
    def _():
        first_lane = jnp.where(lane == 0, 1.0, 0.0).astype(jnp.bfloat16)
        for t in range(length // TILE):
            query_s[t * TILE : (t + 1) * TILE, channels:] = first_lane

    flat = pair_ref[...].reshape(length, channels).astype(jnp.float32)
    normed = layer_norm(flat, gain_ref[...]).astype(jnp.bfloat16)
    projected = jnp.dot(normed, w_ref[...], preferred_element_type=jnp.float32)
    query_s[:, :channels] = (projected[:, :channels] * HEAD_DIM ** (-0.5)).astype(jnp.bfloat16)
    gate_s[...] = jax.nn.sigmoid(projected[:, 3 * channels :])
    for t in range(length // TILE):
        span = slice(t * TILE, (t + 1) * TILE)
        limit = jnp.minimum(counts_ref[row, t], seq_length - t * TILE)
        shown = depth < limit
        hidden = jnp.where(shown, 0.0, masked_score).astype(jnp.bfloat16)
        keys = projected[span, channels : 2 * channels]
        values = projected[span, 2 * channels : 3 * channels]
        for h in range(heads):
            mine = (lane >= h * HEAD_DIM) & (lane < (h + 1) * HEAD_DIM)
            both = mine & shown
            key_s[h, span, :channels] = jnp.where(mine, keys, 0.0).astype(jnp.bfloat16)
            key_s[h, span, channels:] = hidden
            value_s[h, span, :channels] = jnp.where(both, values, 0.0).astype(jnp.bfloat16)
            value_s[h, span, channels:] = jnp.where(both, 1.0, 0.0).astype(jnp.bfloat16)

    size = min(QUERY_TILE, length)
    out_cols = out_ref.shape[2]

    def one_tile(t, carry):
        start = pl.multiple_of(t * size, size)
        span = pl.ds(start, size)
        queries = query_s[span, :]
        total = None
        for h in range(heads):
            scores = dot_nt(queries, key_s[h]) + bias_ref[h, span, :].astype(jnp.float32)
            weights = jnp.exp(scores - jnp.max(scores, axis=-1, keepdims=True))
            term = jnp.dot(
                weights.astype(jnp.bfloat16), value_s[h], preferred_element_type=jnp.float32
            )
            total = term if total is None else total + term
        attended = total[:, :channels] / jnp.maximum(total[:, channels:], 1.0)
        attended = attended.astype(jnp.bfloat16).astype(jnp.float32)
        gated = (gate_s[span, :] * attended).astype(jnp.bfloat16)
        update = jnp.dot(gated, w_out_ref[...], preferred_element_type=jnp.float32)
        update = update.astype(jnp.bfloat16)
        ratio = size // out_cols
        for d in range(ratio):
            out_ref[t * ratio + d, 0] = update[d * out_cols : (d + 1) * out_cols]
        return carry

    lax.fori_loop(0, length // size, one_tile, 0, unroll=UNROLL)


def attention(
    seq_length, counts, pair, gain, weights, w_out, bias, row_base, first, rows, shards
):
    parts, _, cols, channels = pair.shape
    length = parts * cols
    heads = bias.shape[0]
    out_cols = length // shards
    whole = lambda *shape: pl.BlockSpec(
        shape, lambda r: (0,) * len(shape), pipeline_mode=pl.Buffered(1)
    )
    smem = pl.BlockSpec(memory_space=pltpu.SMEM)
    work = rows * heads * length * length
    return pl.pallas_call(
        functools.partial(attention_kernel, row_base=row_base),
        grid=(rows,),
        in_specs=[
            smem,
            smem,
            pl.BlockSpec((parts, 1, cols, channels), lambda r: (0, first + r, 0, 0)),
            whole(1, channels),
            whole(*weights.shape),
            whole(*w_out.shape),
            whole(*bias.shape),
        ],
        out_specs=pl.BlockSpec((shards, 1, out_cols, channels), lambda r: (0, r, 0, 0)),
        out_shape=jax.ShapeDtypeStruct((shards, rows, out_cols, channels), jnp.bfloat16),
        scratch_shapes=[
            pltpu.VMEM((length, 2 * channels), jnp.bfloat16),
            pltpu.VMEM((heads, length, 2 * channels), jnp.bfloat16),
            pltpu.VMEM((heads, length, 2 * channels), jnp.bfloat16),
            pltpu.VMEM((length, channels), jnp.float32),
        ],
        cost_estimate=pl.CostEstimate(
            flops=work * 1024, bytes_accessed=rows * length * channels * 4, transcendentals=work
        ),
        name="row_attention",
    )(seq_length, counts, pair, gain, weights, w_out, bias)


def chunk_sizes(rows):
    sizes = []
    left = rows
    while left > 1 and left > rows // 8:
        take = (left * 3 + 7) // 8
        sizes.append(take)
        left -= take
    return sizes + [left] if left else sizes


def per_device(
    pair, seq_length, tile_counts, ln_gain, w_query, w_key, w_value, w_gate, w_bias, w_out
):
    rows_dev, cols_dev, channels = pair.shape
    key_groups = lax.axis_size("keys")
    head_groups = lax.axis_size("heads")
    shards = key_groups * head_groups
    rows = rows_dev // shards
    heads_dev = w_bias.shape[1]
    heads = heads_dev * head_groups
    length = cols_dev * key_groups
    head_rank = lax.axis_index("heads")
    my_shard = lax.axis_index("keys") * head_groups + head_rank
    gain = ln_gain.reshape(1, channels)

    by_owner = pair.reshape(key_groups, head_groups, rows, cols_dev, channels)
    leaving = lax.dynamic_index_in_dim(by_owner, head_rank, 1, keepdims=False)
    arrived = lax.all_to_all(leaving, "keys", split_axis=0, concat_axis=0, tiled=True)
    counts = lax.dynamic_slice_in_dim(tile_counts, my_shard * rows, rows, 0)

    local = jnp.concatenate([w_query, w_key, w_value, w_gate, w_bias], axis=1)
    gathered = lax.all_gather(local, "heads", axis=0)
    width = w_query.shape[1]
    big = gathered[:, :, : 4 * width].reshape(head_groups, channels, 4, width)
    weights = jnp.transpose(big, (1, 2, 0, 3)).reshape(channels, 4 * width * head_groups)
    bias_t = jnp.transpose(gathered[:, :, 4 * width :], (0, 2, 1)).reshape(heads, channels)
    bias_t = jnp.pad(bias_t, ((0, -heads % 16), (0, 0)))

    share = rows_dev // head_groups
    rank = jnp.reshape(head_rank, (1,)).astype(jnp.int32)
    part = pair_bias_part(pair, rank, share, gain, bias_t)[:heads].reshape(heads, share, cols_dev)
    everyone = lax.all_gather(part, ("rows", "keys", "heads"), axis=0)
    everyone = everyone.reshape(-1, key_groups, head_groups, heads, share, cols_dev)
    bias = jnp.transpose(everyone, (3, 0, 2, 4, 1, 5)).reshape(heads, length, length)

    pieces = []
    done = 0
    for part in chunk_sizes(rows):
        update = attention(
            seq_length, counts, arrived, gain, weights, w_out, bias,
            done, done, part, shards,
        )
        done += part
        pieces.append(
            lax.all_to_all(update, ("keys", "heads"), split_axis=0, concat_axis=0, tiled=True)
        )
    return jnp.concatenate(pieces, axis=1).reshape(rows_dev, length // shards, channels)


def solution(mesh):
    in_specs = (
        P(("groups", "rows"), "keys", None),
        P("groups"),
        P(("groups", "rows"), None),
        P(),
        P(None, "heads"),
        P(None, "heads"),
        P(None, "heads"),
        P(None, "heads"),
        P(None, "heads"),
        P(),
    )
    out_specs = P(("groups", "rows"), ("keys", "heads"), None)
    return jax.shard_map(
        per_device, mesh=mesh, in_specs=in_specs, out_specs=out_specs, check_vma=False
    )
```

profile of v0, /device:TPU:13, one launch (start us, length us, event | category | flops | bytes accessed | tf_op | source)
XLA Modules:
  0.0 232.2 jit_solution(10542403846756997666)
XLA Ops:
  6.5 0.0 copy-start
  6.5 0.0 all-gather.3.cloned.1.call-start
  6.5 0.7 constant_dynamic-update-slice_fusion.4
  7.3 0.7 constant_dynamic-update-slice_fusion.3
  8.0 0.7 constant_dynamic-update-slice_fusion.2
  8.7 0.7 constant_dynamic-update-slice_fusion.1
  9.4 0.7 constant_dynamic-update-slice_fusion
  10.1 2.2 all-gather
  12.3 0.1 reshape.36
  12.5 0.6 pad.4.w_ref
  13.1 8.8 %pair_bias.1 = bf16[16,16384]{1,0:T(8,128)(2,1)} custom-call(s32[1]{0:T(128)} %bitcast.6._, bf16[128,256,128]{2,1,0:T(8,128)(2,1)} %pair_ref.1, f32[1,128]{1,0:T(1,128)} %bitcast.31, bf16[16,128]{1,0:T(8,128)(2,1)} %pad.4.w_ref), custom_call_target="tpu_custom_call" | custom-call | flops 83886080 | bytes 4194304 | tf_op jit(solution)/shard_map/pair_bias/pallas_call | solution.py:41
  21.9 1.0 slice.14
  22.9 0.7 copy.49
  23.5 0.0 all-gather.3.cloned.1.call-update
  23.6 4.7 %dynamic-slice_bitcast_fusion = bf16[2,32,256,128]{3,2,1,0:T(8,128)(2,1)} fusion(bf16[2,2,32,256,128]{4,3,2,1,0:T(8,128)(2,1)} %bitcast.25, s32[]{:T(128)S(6)} %select_n.8), kind=kLoop, calls=%fused_computation | loop fusion | bytes 8388612 | tf_op jit(solution)/shard_map/jit(dynamic_index_in_dim)/squeeze | solution.py:194
  28.3 5.6 %all-to-all-start = ((bf16[2,32,256,128]{3,2,1,0:T(8,128)(2,1)}), bf16[2,32,256,128]{3,2,1,0:T(8,128)(2,1)}, u32[]{:S(2)}, u32[]{:S(2)}) async-start(bf16[2,32,256,128]{3,2,1,0:T(8,128)(2,1)} %dynamic-slice_bitcast_fusion), calls=%async_computation | async-start | bytes 8388608 | tf_op jit(solution)/shard_map/all_to_all | solution.py:195
  33.9 0.1 slice.12
  34.6 0.0 copy-done
  34.7 0.1 constant_dynamic-slice_fusion
  34.7 0.7 copy.45.counts_ref
  35.5 0.8 copy.40.w_ref
  36.2 34.6 %all-gather.3.cloned.1.call-done = bf16[16,4,64,256]{3,2,1,0:T(8,128)(2,1)} async-done(((bf16[1,4,64,256]{3,2,1,0:T(8,128)(2,1)}), bf16[16,4,64,256]{3,2,1,0:T(8,128)(2,1)}) %all-gather.3.cloned.1.call-update) | async-done | bytes 2097168 | tf_op jit(solution)/shard_map/all_gather | solution.py:209
  70.9 3.8 %copy.39 = bf16[4,4,2,64,2,256]{5,4,3,2,1,0:T(2,128)(2,1)S(1)} copy(bf16[4,4,2,64,2,256]{5,3,0,2,4,1:T(8,128)(2,1)} %bitcast.26) | data formatting | bytes 4194304 | tf_op jit(solution)/shard_map/transpose | solution.py:211
  74.7 2.7 %reshape.34.bias_ref = bf16[4,512,512]{2,1,0:T(8,128)(2,1)} reshape(bf16[4,4,2,64,2,256]{5,4,3,2,1,0:T(2,128)(2,1)S(1)} %copy.39) | data formatting | bytes 4194304 | tf_op jit(solution)/shard_map/reshape | solution.py:211
  77.3 9.3 %all-to-all-done.pair_ref = bf16[2,32,256,128]{3,2,1,0:T(8,128)(2,1)} async-done(((bf16[2,32,256,128]{3,2,1,0:T(8,128)(2,1)}), bf16[2,32,256,128]{3,2,1,0:T(8,128)(2,1)}, u32[]{:S(2)}, u32[]{:S(2)}) %all-to-all-start) | async-done | bytes 4194336 | tf_op jit(solution)/shard_map/all_to_all | solution.py:195
  86.6 10.9 %row_attention.8 = bf16[4,3,128,128]{3,2,1,0:T(8,128)(2,1)} custom-call(s32[1]{0:T(128)S(6)} %copy.58.seq_ref, s32[32,4]{1,0:T(8,128)} %copy.45.counts_ref, bf16[2,32,256,128]{3,2,1,0:T(8,128)(2,1)} %all-to-all-done.pair_ref, f32[1,128]{1,0:T(1,128)} %bitcast.32, bf16[128,512]{1,0:T(8,128)(2,1)} %copy.40.w_ref, bf16[128,128]{1,0:T(8,128)(2,1)} %w_out_ref.9, ...), custom_call_target="tpu_custom_call" | custom-call | flops 3221225472 | bytes 786432 | tf_op jit(solution)/shard_map/row_attention/pallas_call | solution.py:141
  97.5 4.6 %all-to-all-start.4 = ((bf16[4,3,128,128]{3,2,1,0:T(8,128)(2,1)}), bf16[4,3,128,128]{3,2,1,0:T(8,128)(2,1)S(1)}, u32[]{:S(2)}, u32[]{:S(2)}) async-start(bf16[4,3,128,128]{3,2,1,0:T(8,128)(2,1)} %row_attention.8), calls=%async_computation.4 | async-start | bytes 786432 | tf_op jit(solution)/shard_map/all_to_all | solution.py:222
  102.1 16.5 %row_attention.7 = bf16[4,5,128,128]{3,2,1,0:T(8,128)(2,1)} custom-call(s32[1]{0:T(128)S(6)} %copy.58.seq_ref, s32[32,4]{1,0:T(8,128)} %copy.45.counts_ref, bf16[2,32,256,128]{3,2,1,0:T(8,128)(2,1)} %all-to-all-done.pair_ref, f32[1,128]{1,0:T(1,128)} %bitcast.33, bf16[128,512]{1,0:T(8,128)(2,1)} %copy.40.w_ref, bf16[128,128]{1,0:T(8,128)(2,1)} %w_out_ref.9, ...), custom_call_target="tpu_custom_call" | custom-call | flops 5368709120 | bytes 1310720 | tf_op jit(solution)/shard_map/row_attention/pallas_call | solution.py:141
  118.6 0.0 all-to-all-done.4
  118.6 0.0 copy-start.1
  118.6 0.7 copy-done.1
  119.4 3.7 %all-to-all-start.3 = ((bf16[4,5,128,128]{3,2,1,0:T(8,128)(2,1)}), bf16[4,5,128,128]{3,2,1,0:T(8,128)(2,1)S(1)}, u32[]{:S(2)}, u32[]{:S(2)}) async-start(bf16[4,5,128,128]{3,2,1,0:T(8,128)(2,1)} %row_attention.7), calls=%async_computation.3 | async-start | bytes 1310720 | tf_op jit(solution)/shard_map/all_to_all | solution.py:222
  123.0 25.0 %row_attention.6 = bf16[4,8,128,128]{3,2,1,0:T(8,128)(2,1)} custom-call(s32[1]{0:T(128)S(6)} %copy.58.seq_ref, s32[32,4]{1,0:T(8,128)} %copy.45.counts_ref, bf16[2,32,256,128]{3,2,1,0:T(8,128)(2,1)} %all-to-all-done.pair_ref, f32[1,128]{1,0:T(1,128)} %bitcast.34, bf16[128,512]{1,0:T(8,128)(2,1)} %copy.40.w_ref, bf16[128,128]{1,0:T(8,128)(2,1)} %w_out_ref.9, ...), custom_call_target="tpu_custom_call" | custom-call | flops 8589934592 | bytes 2097152 | tf_op jit(solution)/shard_map/row_attention/pallas_call | solution.py:141
  148.0 0.0 all-to-all-done.3
  148.0 3.6 %all-to-all-start.2 = ((bf16[4,8,128,128]{3,2,1,0:T(8,128)(2,1)}), bf16[4,8,128,128]{3,2,1,0:T(8,128)(2,1)S(1)}, u32[]{:S(2)}, u32[]{:S(2)}) async-start(bf16[4,8,128,128]{3,2,1,0:T(8,128)(2,1)} %row_attention.6), calls=%async_computation.2 | async-start | bytes 2097152 | tf_op jit(solution)/shard_map/all_to_all | solution.py:222
  151.5 36.2 %row_attention.5 = bf16[4,12,128,128]{3,2,1,0:T(8,128)(2,1)} custom-call(s32[1]{0:T(128)S(6)} %copy.58.seq_ref, s32[32,4]{1,0:T(8,128)} %copy.45.counts_ref, bf16[2,32,256,128]{3,2,1,0:T(8,128)(2,1)} %all-to-all-done.pair_ref, f32[1,128]{1,0:T(1,128)} %bitcast.35, bf16[128,512]{1,0:T(8,128)(2,1)} %copy.40.w_ref, bf16[128,128]{1,0:T(8,128)(2,1)} %w_out_ref.9, ...), custom_call_target="tpu_custom_call" | custom-call | flops 12884901888 | bytes 3145728 | tf_op jit(solution)/shard_map/row_attention/pallas_call | solution.py:141
  187.7 0.0 all-to-all-done.2
  187.7 3.6 %all-to-all-start.1 = ((bf16[4,12,128,128]{3,2,1,0:T(8,128)(2,1)}), bf16[4,12,128,128]{3,2,1,0:T(8,128)(2,1)S(1)}, u32[]{:S(2)}, u32[]{:S(2)}) async-start(bf16[4,12,128,128]{3,2,1,0:T(8,128)(2,1)} %row_attention.5), calls=%async_computation.1 | async-start | bytes 3145728 | tf_op jit(solution)/shard_map/all_to_all | solution.py:222
  191.3 13.7 %row_attention.9 = bf16[4,4,128,128]{3,2,1,0:T(8,128)(2,1)} custom-call(s32[1]{0:T(128)S(6)} %copy.58.seq_ref, s32[32,4]{1,0:T(8,128)} %copy.45.counts_ref, bf16[2,32,256,128]{3,2,1,0:T(8,128)(2,1)} %all-to-all-done.pair_ref, f32[1,128]{1,0:T(1,128)} %bitcast.36, bf16[128,512]{1,0:T(8,128)(2,1)} %copy.40.w_ref, bf16[128,128]{1,0:T(8,128)(2,1)} %w_out_ref.9, ...), custom_call_target="tpu_custom_call" | custom-call | flops 4294967296 | bytes 1048576 | tf_op jit(solution)/shard_map/row_attention/pallas_call | solution.py:141
  205.0 5.4 %all-to-all-done.1 = bf16[4,12,128,128]{3,2,1,0:T(8,128)(2,1)S(1)} async-done(((bf16[4,12,128,128]{3,2,1,0:T(8,128)(2,1)}), bf16[4,12,128,128]{3,2,1,0:T(8,128)(2,1)S(1)}, u32[]{:S(2)}, u32[]{:S(2)}) %all-to-all-start.1) | async-done | bytes 1572896 | tf_op jit(solution)/shard_map/all_to_all | solution.py:222
  210.4 5.1 %all-to-all-start.5 = ((bf16[4,4,128,128]{3,2,1,0:T(8,128)(2,1)}), bf16[4,4,128,128]{3,2,1,0:T(8,128)(2,1)}, u32[]{:S(2)}, u32[]{:S(2)}) async-start(bf16[4,4,128,128]{3,2,1,0:T(8,128)(2,1)} %row_attention.9), calls=%async_computation.5 | async-start | bytes 1048576 | tf_op jit(solution)/shard_map/all_to_all | solution.py:222
  215.5 1.4 constant_dynamic-update-slice_fusion.9
  216.9 1.2 constant_dynamic-update-slice_fusion.8
  218.0 0.9 constant_dynamic-update-slice_fusion.7
  219.0 0.0 copy-done.2
  219.0 0.8 constant_dynamic-update-slice_fusion.6
  219.8 3.6 %all-to-all-done.5 = bf16[4,4,128,128]{3,2,1,0:T(8,128)(2,1)} async-done(((bf16[4,4,128,128]{3,2,1,0:T(8,128)(2,1)}), bf16[4,4,128,128]{3,2,1,0:T(8,128)(2,1)}, u32[]{:S(2)}, u32[]{:S(2)}) %all-to-all-start.5) | async-done | bytes 524320 | tf_op jit(solution)/shard_map/all_to_all | solution.py:222
  223.4 2.0 constant_dynamic-update-slice_fusion.5
  (5 shorter events, 0.0 us)
Async XLA Ops:
  6.5 28.1 %copy-start = (s32[128,4]{0,1:T(4,128)S(1)}, s32[128,4]{0,1:T(4,128)}, u32[]{:S(2)}) copy-start(s32[128,4]{0,1:T(4,128)} %param.12) | copy-start | bytes 6148
  6.5 64.3 %all-gather.3.cloned.1.call-start = ((), (), s32[]{:S(2)}) async-start(), calls=%async_computation.6 | async-start | bytes 2228224 | tf_op jit(solution)/shard_map/all_gather | solution.py:209
  28.3 58.4 %all-to-all-start = ((bf16[2,32,256,128]{3,2,1,0:T(8,128)(2,1)}), bf16[2,32,256,128]{3,2,1,0:T(8,128)(2,1)}, u32[]{:S(2)}, u32[]{:S(2)}) async-start(bf16[2,32,256,128]{3,2,1,0:T(8,128)(2,1)} %dynamic-slice_bitcast_fusion), calls=%async_computation | async-start | bytes 8388608 | tf_op jit(solution)/shard_map/all_to_all | solution.py:195
  97.5 21.1 %all-to-all-start.4 = ((bf16[4,3,128,128]{3,2,1,0:T(8,128)(2,1)}), bf16[4,3,128,128]{3,2,1,0:T(8,128)(2,1)S(1)}, u32[]{:S(2)}, u32[]{:S(2)}) async-start(bf16[4,3,128,128]{3,2,1,0:T(8,128)(2,1)} %row_attention.8), calls=%async_computation.4 | async-start | bytes 786432 | tf_op jit(solution)/shard_map/all_to_all | solution.py:222
  118.6 0.7 copy-start.1
  119.4 28.6 %all-to-all-start.3 = ((bf16[4,5,128,128]{3,2,1,0:T(8,128)(2,1)}), bf16[4,5,128,128]{3,2,1,0:T(8,128)(2,1)S(1)}, u32[]{:S(2)}, u32[]{:S(2)}) async-start(bf16[4,5,128,128]{3,2,1,0:T(8,128)(2,1)} %row_attention.7), calls=%async_computation.3 | async-start | bytes 1310720 | tf_op jit(solution)/shard_map/all_to_all | solution.py:222
  148.0 39.7 %all-to-all-start.2 = ((bf16[4,8,128,128]{3,2,1,0:T(8,128)(2,1)}), bf16[4,8,128,128]{3,2,1,0:T(8,128)(2,1)S(1)}, u32[]{:S(2)}, u32[]{:S(2)}) async-start(bf16[4,8,128,128]{3,2,1,0:T(8,128)(2,1)} %row_attention.6), calls=%async_computation.2 | async-start | bytes 2097152 | tf_op jit(solution)/shard_map/all_to_all | solution.py:222
  187.7 22.7 %all-to-all-start.1 = ((bf16[4,12,128,128]{3,2,1,0:T(8,128)(2,1)}), bf16[4,12,128,128]{3,2,1,0:T(8,128)(2,1)S(1)}, u32[]{:S(2)}, u32[]{:S(2)}) async-start(bf16[4,12,128,128]{3,2,1,0:T(8,128)(2,1)} %row_attention.5), calls=%async_computation.1 | async-start | bytes 3145728 | tf_op jit(solution)/shard_map/all_to_all | solution.py:222
  210.4 13.0 %all-to-all-start.5 = ((bf16[4,4,128,128]{3,2,1,0:T(8,128)(2,1)}), bf16[4,4,128,128]{3,2,1,0:T(8,128)(2,1)}, u32[]{:S(2)}, u32[]{:S(2)}) async-start(bf16[4,4,128,128]{3,2,1,0:T(8,128)(2,1)} %row_attention.9), calls=%async_computation.5 | async-start | bytes 1048576 | tf_op jit(solution)/shard_map/all_to_all | solution.py:222
  215.5 3.5 %copy-start.2 = (bf16[4,3,128,128]{3,2,1,0:T(8,128)(2,1)S(1)}, bf16[4,3,128,128]{3,2,1,0:T(8,128)(2,1)}, u32[]{:S(2)}) copy-start(bf16[4,3,128,128]{3,2,1,0:T(8,128)(2,1)} %copy-done.1) | copy-start | bytes 1179652
Sparse Core Ops, SparseCore 0:
  23.7 47.1 all-gather.2
where the time goes:
time: 235 us; the launch traced here: 232 us
  Pallas kernels  111 us (47%)
  waiting for transfers between devices  53 us (23%)
  starting transfers between devices  26.1 us (11%)
  local copies, waits for them, and re-layouts  25.8 us (11%)
  between operations  14.1 us (6%)
    pallas_call x5, Pallas kernels, attention(): pl.pallas_call(functools.partial(attention_kernel, row_base=row_base), gr...  102 us
    all_gather x1, waiting for transfers between devices, per_device(): everyone = lax.all_gather(part, ('rows', 'keys', 'heads'), axis=0)  34.6 us
    all_to_all x5, starting transfers between devices, per_device(): lax.all_to_all(update, ('keys', 'heads'), split_axis=0, concat_axis=0, ti...  20.5 us
    unnamed x16, local copies, waits for them, and re-layouts  9.35 us
    all_to_all x1, waiting for transfers between devices, per_device(): lax.all_to_all(leaving, 'keys', split_axis=0, concat_axis=0, tiled=True)  9.31 us
    all_to_all x5, waiting for transfers between devices, per_device(): lax.all_to_all(update, ('keys', 'heads'), split_axis=0, concat_axis=0, ti...  9.05 us
    pallas_call x1, Pallas kernels, pair_bias_part(): pl.pallas_call(bias_kernel, grid_spec=pltpu.PrefetchScalarGridSpec(num_sc...  8.78 us
    all_to_all x1, starting transfers between devices, per_device(): lax.all_to_all(leaving, 'keys', split_axis=0, concat_axis=0, tiled=True)  5.61 us
  transfers between devices with their start and end apart: 7, of which 4 were waited for; matrix products, arithmetic and copies ran while one was open for 7% of the time, Pallas kernels for 39%

commit v1 on v0

v1 whole, which is shorter than its diff:
```python
import functools
import math

import jax
import jax.numpy as jnp
from jax import lax
from jax.experimental import pallas as pl
from jax.experimental.pallas import tpu as pltpu
from jax.sharding import PartitionSpec as P

HEAD_DIM = 32
TILE = 128
LOG2E = math.log2(math.e)
ROWS_OF_64 = (20, 24, 20)

norm_epsilon = 1e-05
masked_score = -1e30


def layer_norm(values, gain):
    center = values - jnp.mean(values, axis=-1, keepdims=True)
    spread = jnp.mean(center * center, axis=-1, keepdims=True)
    return center * lax.rsqrt(spread + norm_epsilon) * gain


def dot_nt(a, b):
    return lax.dot_general(a, b, (((1,), (1,)), ((), ())), preferred_element_type=jnp.float32)


def dot_tn(a, b):
    return lax.dot_general(a, b, (((0,), (0,)), ((), ())), preferred_element_type=jnp.float32)


def bias_kernel(_, pair_ref, gain_ref, w_ref, out_ref, by_row):
    rows, cols, channels = pair_ref.shape
    padded = by_row.shape[1]
    step = pl.program_id(0)
    flat = pair_ref[...].reshape(rows * cols, channels).astype(jnp.float32)
    normed = layer_norm(flat, gain_ref[...]).astype(jnp.bfloat16)
    found = dot_nt(w_ref[...], normed)
    for r in range(rows):
        by_row[step * rows + r] = found[:padded, r * cols : (r + 1) * cols]

    @pl.when(step == pl.num_programs(0) - 1)
    def _():
        for h in range(out_ref.shape[0]):
            out_ref[h] = (by_row[:, h, :] * LOG2E).astype(jnp.bfloat16)


def pair_bias_part(pair, core, cols, gain, w_bias_t, heads):
    rows, _, channels = pair.shape
    block = min(rows, 16)
    padded = -(-heads // 8) * 8
    return pl.pallas_call(
        bias_kernel,
        grid_spec=pltpu.PrefetchScalarGridSpec(
            num_scalar_prefetch=1,
            grid=(rows // block,),
            in_specs=[
                pl.BlockSpec((block, cols, channels), lambda r, which: (r, which[0], 0)),
                pl.BlockSpec((1, channels), lambda r, which: (0, 0)),
                pl.BlockSpec(w_bias_t.shape, lambda r, which: (0, 0)),
            ],
            out_specs=pl.BlockSpec((heads, rows, cols), lambda r, which: (0, 0, 0)),
            scratch_shapes=[pltpu.VMEM((rows, padded, cols), jnp.float32)],
        ),
        out_shape=jax.ShapeDtypeStruct((heads, rows, cols), jnp.bfloat16),
        cost_estimate=pl.CostEstimate(
            flops=rows * cols * channels * 200, bytes_accessed=rows * cols * channels * 2,
            transcendentals=0,
        ),
        name="pair_bias",
    )(core, pair, gain, w_bias_t)


def row_limits(counts_ref, row, seq, parts, tiles):
    limits = []
    for part in parts:
        for t in range(tiles):
            g = part * tiles + t
            limits.append(jnp.minimum(counts_ref[row, g], seq - g * TILE))
    return limits, functools.reduce(jnp.maximum, limits)


def own_kernel(info_ref, seq_ref, counts_ref, pair_ref, gain_ref, w_ref, kv_ref, q_ref, gate_ref, *, parts):
    rows, cols, channels = pair_ref.shape
    step = pl.program_id(0)
    order = [info_ref[1 + p] for p in range(parts)]
    most = [
        row_limits(counts_ref, step * rows + r, seq_ref[0], order, cols // TILE)[1]
        for r in range(rows)
    ]

    @pl.when(functools.reduce(jnp.maximum, most) > 0)
    def _():
        flat = pair_ref[...].reshape(rows * cols, channels).astype(jnp.float32)
        normed = layer_norm(flat, gain_ref[...]).astype(jnp.bfloat16)
        found = jnp.dot(normed, w_ref[...], preferred_element_type=jnp.float32)
        found = found.reshape(rows, cols, 4 * channels)
        kv_ref[...] = found[:, :, : 2 * channels].astype(jnp.bfloat16)
        scale = HEAD_DIM ** -0.5 * LOG2E
        q_ref[...] = (found[:, :, 2 * channels : 3 * channels] * scale).astype(jnp.bfloat16)
        gate_ref[...] = jax.nn.sigmoid(found[:, :, 3 * channels :])


def own_rows(info, seq_length, counts, pair, gain, w, parts):
    _, cols, channels = pair.shape
    rows = counts.shape[0]
    block = 2 if rows % 2 == 0 else 1
    steps = rows // block
    spec = lambda width: pl.BlockSpec((block, cols, width), lambda r, *_: (r, 0, 0))
    return pl.pallas_call(
        functools.partial(own_kernel, parts=parts),
        grid_spec=pltpu.PrefetchScalarGridSpec(
            num_scalar_prefetch=3,
            grid=(steps,),
            in_specs=[
                pl.BlockSpec((block, cols, channels), lambda r, info, *_: (info[0] * steps + r, 0, 0)),
                pl.BlockSpec(gain.shape, lambda r, *_: (0, 0)),
                pl.BlockSpec(w.shape, lambda r, *_: (0, 0)),
            ],
            out_specs=[spec(2 * channels), spec(channels), spec(channels)],
        ),
        out_shape=[
            jax.ShapeDtypeStruct((rows, cols, 2 * channels), jnp.bfloat16),
            jax.ShapeDtypeStruct((rows, cols, channels), jnp.bfloat16),
            jax.ShapeDtypeStruct((rows, cols, channels), jnp.float32),
        ],
        cost_estimate=pl.CostEstimate(
            flops=rows * cols * channels * 8000, bytes_accessed=rows * cols * channels * 12,
            transcendentals=rows * cols * channels,
        ),
        name="own_rows",
    )(info, seq_length, counts, pair, gain, w)


def attention_kernel(info_ref, seq_ref, counts_ref, *refs, others, base, rows):
    kv_ref, q_ref, gate_ref = refs[:3]
    pairs = refs[3 : 3 + others]
    gain_ref, wk_ref, wo_ref, blocks_ref = refs[3 + others : 7 + others]
    mine_ref, theirs_ref, bias_ref = refs[-9:-6]
    slots = (refs[-6:-3], refs[-3:])
    _, cols, channels = q_ref.shape
    heads = bias_ref.shape[0]
    step = pl.program_id(0)
    tiles = cols // TILE
    length = (1 + others) * cols
    width = mine_ref.shape[1]
    shards = cols // width
    core = info_ref[0]
    order = [info_ref[1 + p] for p in range(1 + others)]
    seq = seq_ref[0]
    coming, most = row_limits(counts_ref, base + jnp.minimum(step, rows - 1), seq, order, tiles)
    _, least = row_limits(counts_ref, base + jnp.maximum(step - 1, 0), seq, order, tiles)
    project_now = (most > 0) & (step < rows)
    attend_now = (least > 0) & (step > 0)
    even = lax.rem(step, 2) == 0

    @pl.when(step == 0)
    def _():
        lane = lax.broadcasted_iota(jnp.int32, (cols, channels), 1)
        for _, query_s, value_s in slots:
            for h in range(heads):
                hide = jnp.where(lane == 0, masked_score, 0.0)
                query_s[h, :, channels:] = hide.astype(jnp.bfloat16)
            value_s[:, channels:] = jnp.ones((length, channels), jnp.bfloat16)
        halves, needed, parts, _, part_rows, part_cols = blocks_ref.shape
        for n in range(needed):
            down = slice(n * part_rows, (n + 1) * part_rows)
            for p in range(parts):
                for c in range(halves):
                    first = p * cols + c * part_cols
                    block = blocks_ref[c, n, p].astype(jnp.float32)
                    bias_ref[:, down, first : first + part_cols] = block

    def project(slot):
        key_s, query_s, value_s = slot
        lane = lax.broadcasted_iota(jnp.int32, (cols, channels), 1)
        depth = lax.broadcasted_iota(jnp.int32, (TILE, channels), 0)
        q = q_ref[0]
        for h in range(heads):
            mine = (lane >= h * HEAD_DIM) & (lane < (h + 1) * HEAD_DIM)
            query_s[h, :, :channels] = jnp.where(mine, q.astype(jnp.float32), 0.0).astype(jnp.bfloat16)
        key_s[:cols, :channels] = kv_ref[0, :, :channels]
        value_s[:cols, :channels] = kv_ref[0, :, channels:]
        for p in range(1 + others):
            for t in range(tiles):
                hidden = jnp.where(depth < coming[p * tiles + t], 0.0, 1.0).astype(jnp.bfloat16)
                first = p * cols + t * TILE
                key_s[first : first + TILE, channels:] = hidden
        for p in range(others):
            span = slice((p + 1) * cols, (p + 2) * cols)
            normed = layer_norm(pairs[p][0].astype(jnp.float32), gain_ref[...])
            kv = jnp.dot(normed.astype(jnp.bfloat16), wk_ref[...], preferred_element_type=jnp.float32)
            key_s[span, :channels] = kv[:, :channels].astype(jnp.bfloat16)
            value_s[span, :channels] = kv[:, channels:].astype(jnp.bfloat16)

    def attend(slot):
        key_s, query_s, value_s = slot
        lane = lax.broadcasted_iota(jnp.int32, (cols, channels), 1)
        stacked = query_s[...].reshape(heads * cols, 2 * channels)
        every = dot_nt(stacked, key_s[...])
        for h in range(heads):
            scores = every[h * cols : (h + 1) * cols] + bias_ref[h]
            weights = jnp.exp2(scores - jnp.max(scores, axis=-1, keepdims=True))
            mixed = jnp.dot(
                weights.astype(jnp.bfloat16), value_s[...], preferred_element_type=jnp.float32
            )
            if h == 0:
                top, low = mixed[:, :channels], mixed[:, channels:]
            else:
                later = lane >= h * HEAD_DIM
                top = jnp.where(later, mixed[:, :channels], top)
                low = jnp.where(later, mixed[:, channels:], low)
        attended = (top / jnp.maximum(low, 1.0)).astype(jnp.bfloat16).astype(jnp.float32)
        gated = (gate_ref[0] * attended).astype(jnp.bfloat16)
        update = jnp.dot(gated, wo_ref[...], preferred_element_type=jnp.float32)
        update = update.astype(jnp.bfloat16)
        for d in range(shards):
            part = update[d * width : (d + 1) * width]

            @pl.when(core == d)
            def _():
                mine_ref[0] = part

            @pl.when(core != d)
            def _():
                theirs_ref[lax.rem(d + shards - core, shards) - 1, 0] = part

    for parity in range(2):
        turn = even if parity == 0 else ~even

        @pl.when(turn & project_now & attend_now)
        def _():
            attend(slots[1 - parity])
            project(slots[parity])

        @pl.when(turn & project_now & ~attend_now)
        def _():
            project(slots[parity])

        @pl.when(turn & ~project_now & attend_now)
        def _():
            attend(slots[1 - parity])

    @pl.when(~attend_now)
    def _():
        mine_ref[...] = jnp.zeros_like(mine_ref)
        theirs_ref[...] = jnp.zeros_like(theirs_ref)


def attention(info, seq_length, counts, own, pairs, gain, wk, wo, bias, out, base, rows, shards):
    kv, q, gate = own
    _, cols, channels = q.shape
    others = len(pairs)
    heads = bias.shape[3]
    length = bias.shape[2] * cols
    all_rows = kv.shape[0]
    last = rows - 1
    whole = lambda a: pl.BlockSpec(
        a.shape, lambda r, *_: (0,) * a.ndim, pipeline_mode=pl.Buffered(1)
    )
    work = rows * heads * length * cols
    width = cols // shards
    now = lambda r: jnp.minimum(r, last)
    past = lambda r: jnp.maximum(r - 1, 0)
    bf = jnp.bfloat16
    slot = [
        pltpu.VMEM((length, 2 * channels), bf),
        pltpu.VMEM((heads, cols, 2 * channels), bf),
        pltpu.VMEM((length, 2 * channels), bf),
    ]
    return pl.pallas_call(
        functools.partial(attention_kernel, others=others, base=base, rows=rows),
        grid_spec=pltpu.PrefetchScalarGridSpec(
            num_scalar_prefetch=3,
            grid=(rows + 1,),
            in_specs=[
                pl.BlockSpec((1, cols, 2 * channels), lambda r, *_: (base + now(r), 0, 0)),
                pl.BlockSpec((1, cols, channels), lambda r, *_: (base + now(r), 0, 0)),
                pl.BlockSpec((1, cols, channels), lambda r, *_: (base + past(r), 0, 0)),
            ]
            + [pl.BlockSpec((1, cols, channels), lambda r, *_: (now(r), 0, 0))] * others
            + [whole(a) for a in (gain, wk, wo, bias)]
            + [pl.BlockSpec(memory_space=pl.ANY)] * len(out),
            out_specs=[
                pl.BlockSpec(
                    (1, width, channels),
                    lambda r, info, *_: (info[0] * all_rows + base + past(r), 0, 0),
                ),
                pl.BlockSpec((shards - 1, 1, width, channels), lambda r, *_: (0, past(r), 0, 0)),
            ],
            scratch_shapes=[pltpu.VMEM((heads, cols, length), jnp.float32)] + slot * 2,
        ),
        out_shape=[
            jax.ShapeDtypeStruct((all_rows * shards, width, channels), bf),
            jax.ShapeDtypeStruct((shards - 1, rows, width, channels), bf),
        ],
        input_output_aliases={10 + others: 0} if out else {},
        cost_estimate=pl.CostEstimate(
            flops=work * 1024, bytes_accessed=rows * length * channels * 4, transcendentals=work
        ),
        name="row_attention",
    )(info, seq_length, counts, kv, q, gate, *pairs, gain, wk, wo, bias, *out)


def split_rows(rows):
    sizes = []
    left = rows
    for part in ROWS_OF_64[:-1]:
        take = min(left, max(1, rows * part // 64))
        if take:
            sizes.append(take)
        left -= take
    if left:
        sizes.append(left)
    return sizes


def rotate(x, axis, shift):
    size = lax.axis_size(axis)
    return lax.ppermute(x, axis, [(i, (i + shift) % size) for i in range(size)])


def gather_bias(part, own, key_groups, head_groups, row_groups):
    heads, rows, span = part.shape
    x = lax.axis_index("keys")
    z = lax.axis_index("rows")
    core = lax.axis_index("heads")
    by_keys = jnp.stack([part] + [rotate(part, "keys", s) for s in range(1, key_groups)])
    needed = row_groups // key_groups
    if row_groups <= 8:
        blocks = [by_keys]
        for s in range(1, row_groups):
            pairs = []
            for zz in range(row_groups):
                xx = zz // needed
                dest = (zz + s) % row_groups
                pairs.append((zz * key_groups + xx, dest * key_groups + xx))
            blocks.append(lax.ppermute(by_keys, ("rows", "keys"), pairs))
        blocks, own = lax.optimization_barrier((blocks, own))
        blocks = jnp.stack(blocks)
        mine = [
            lax.dynamic_index_in_dim(
                blocks, lax.rem(z - (x * needed + n) + row_groups, row_groups), 0, False
            )
            for n in range(needed)
        ]
        mine = jnp.stack(mine)
    else:
        every = lax.all_gather(by_keys, "rows", axis=0)
        mine = lax.dynamic_slice_in_dim(every, x * needed, needed, 0)
    cores = jnp.stack([mine] + [rotate(mine, "heads", s) for s in range(1, head_groups)])
    ordered = [
        lax.dynamic_index_in_dim(cores, lax.rem(core - c + head_groups, head_groups), 0, False)
        for c in range(head_groups)
    ]
    return jnp.stack(ordered), own


def per_device(
    pair, seq_length, tile_counts, ln_gain, w_query, w_key, w_value, w_gate, w_bias, w_out
):
    rows_dev, cols_dev, channels = pair.shape
    key_groups = lax.axis_size("keys")
    head_groups = lax.axis_size("heads")
    row_groups = lax.axis_size("rows")
    rows = rows_dev // head_groups
    heads = w_bias.shape[1] * head_groups
    core = lax.axis_index("heads")
    x = lax.axis_index("keys")
    gain = ln_gain.reshape(1, channels)

    sizes = split_rows(rows)
    starts = [sum(sizes[:i]) for i in range(len(sizes))]

    local = jnp.concatenate([w_query, w_key, w_value, w_gate, w_bias], axis=1)
    gathered = lax.all_gather(local, "heads", axis=0)
    width = w_query.shape[1]
    big = gathered[:, :, : 4 * width].reshape(head_groups, channels, 4, width)
    big = jnp.transpose(big, (2, 1, 0, 3)).reshape(4, channels, width * head_groups)
    w_all = jnp.concatenate([big[1], big[2], big[0], big[3]], axis=1)
    bias_t = jnp.transpose(gathered[:, :, 4 * width :], (0, 2, 1)).reshape(heads, channels)
    bias_t = jnp.pad(bias_t, ((0, -heads % 16), (0, 0)))

    core_1 = jnp.reshape(core, (1,)).astype(jnp.int32)
    part = pair_bias_part(pair, core_1, cols_dev // head_groups, gain, bias_t, heads)

    arrived = []
    source = pair
    for i, (start, size) in enumerate(zip(starts, sizes)):
        if i == 1:
            source, _ = lax.optimization_barrier((pair, part))
        piece = lax.dynamic_slice_in_dim(source, core * rows + start, size, 0)
        arrived.append([rotate(piece, "keys", s) for s in range(1, key_groups)])

    counts = lax.dynamic_slice_in_dim(tile_counts, core * rows, rows, 0)
    info = jnp.stack([core] + [lax.rem(x - s + key_groups, key_groups) for s in range(key_groups)])
    info = info.astype(jnp.int32)
    own = own_rows(info, seq_length, counts, pair, gain, w_all, key_groups)
    bias, own = gather_bias(part, own, key_groups, head_groups, row_groups)

    out = []
    swapped = []
    for i, (start, size) in enumerate(zip(starts, sizes)):
        mine, theirs = attention(
            info, seq_length, counts, own, arrived[i], gain, w_all[:, : 2 * channels], w_out, bias,
            out, start, size, head_groups,
        )
        out = [mine]
        swapped.append([rotate(theirs[s - 1], "heads", s) for s in range(1, head_groups)])
    out = out[0]
    for start, others in zip(starts, swapped):
        for s, other in enumerate(others, 1):
            owner = lax.rem(core - s + head_groups, head_groups)
            out = lax.dynamic_update_slice(out, other, (owner * rows + start, 0, 0))
    return out


def solution(mesh):
    in_specs = (
        P(("groups", "rows"), "keys", None),
        P("groups"),
        P(("groups", "rows"), None),
        P(),
        P(None, "heads"),
        P(None, "heads"),
        P(None, "heads"),
        P(None, "heads"),
        P(None, "heads"),
        P(),
    )
    out_specs = P(("groups", "rows"), ("keys", "heads"), None)
    return jax.shard_map(
        per_device, mesh=mesh, in_specs=in_specs, out_specs=out_specs, check_vma=False
    )
```

time: 235 us -> 184 us (0.78)
  waiting for transfers between devices: 53 us -> 0.12 us
  Pallas kernels: 111 us -> 141 us
  between operations: 14.1 us -> 0.83 us
  local copies, waits for them, and re-layouts: 25.8 us -> 14 us
  starting transfers between devices: 26.1 us -> 16.9 us
  other arithmetic: 0 us -> 6.33 us
    all_gather x1 -> x0, waiting for transfers between devices: 34.6 us -> none  [per_device(): everyone = lax.all_gather(part, ('rows', 'keys', 'heads'), axis=0)]
    pallas_call x5 -> x4, Pallas kernels: 102 us -> 132 us  [the longest x3 102 us: attention(): pl.pallas_call(functools.partial(attention_kernel, others=others, base=ba...]
    all_to_all x6 -> x0, starting transfers between devices: 26.1 us -> none  [the longest x5 20.5 us: per_device(): lax.all_to_all(update, ('keys', 'heads'), split_axis=0, concat_axis=0, ti...]
    all_to_all x6 -> x0, waiting for transfers between devices: 18.4 us -> none  [the longest x1 9.31 us: per_device(): lax.all_to_all(leaving, 'keys', split_axis=0, concat_axis=0, tiled=True)]
    ppermute x0 -> x11, starting transfers between devices: none -> 16.9 us  [the longest x8 9.13 us: rotate(): return lax.ppermute(x, axis, [(i, (i + shift) % size) for i in range(size)])]
    unnamed x16 -> x7, local copies, waits for them, and re-layouts: 9.35 us -> 3.6 us
    dynamic_slice x1 -> x5, local copies, waits for them, and re-layouts: 0.07 us -> 5.66 us  [the longest x3 5.54 us: per_device(): piece = lax.dynamic_slice_in_dim(source, core * rows + start, size, 0)]
    another operation x0 -> x6, other arithmetic: none -> 5.03 us  [the longest x1 1.42 us: gather_bias(): jnp.stack([mine] + [rotate(mine, 'heads', s) for s in range(1, head_group...]
  transfers between devices with their start and end apart: 7 -> 11, of which waited for: 4 -> 1; matrix products, arithmetic and copies ran while one was open for 7% -> 8% of each run, Pallas kernels for 39% -> 73%
where the time goes in v1:
time: 184 us; the launch traced here: 181 us
  Pallas kernels  141 us (77%)
  starting transfers between devices  16.9 us (9%)
  local copies, waits for them, and re-layouts  14 us (8%)
  other arithmetic  6.33 us (3%)
  blocking collectives  2.24 us (1%)
    pallas_call x3, Pallas kernels, attention(): pl.pallas_call(functools.partial(attention_kernel, others=others, base=ba...  102 us
    pallas_call x1, Pallas kernels, own_rows(): pl.pallas_call(functools.partial(own_kernel, parts=parts), grid_spec=pltp...  29.8 us
    ppermute x8, starting transfers between devices, rotate(): return lax.ppermute(x, axis, [(i, (i + shift) % size) for i in range(size)])  9.13 us
    pallas_call x1, Pallas kernels, pair_bias_part(): pl.pallas_call(bias_kernel, grid_spec=pltpu.PrefetchScalarGridSpec(num_sc...  9.07 us
    ppermute x3, starting transfers between devices, gather_bias(): blocks.append(lax.ppermute(by_keys, ('rows', 'keys'), pairs))  7.79 us
    dynamic_slice x3, local copies, waits for them, and re-layouts, per_device(): piece = lax.dynamic_slice_in_dim(source, core * rows + start, size, 0)  5.54 us
  transfers between devices with their start and end apart: 11, of which 1 were waited for; matrix products, arithmetic and copies ran while one was open for 8% of the time, Pallas kernels for 73%

profile of v1, /device:TPU:13, one launch (start us, length us, event | category | flops | bytes accessed | tf_op | source)
XLA Modules:
  0.0 181.3 jit_solution(13759493275423829347)
XLA Ops:
  0.0 0.7 constant_dynamic-update-slice_fusion.4
  0.7 0.7 constant_dynamic-update-slice_fusion.3
  1.5 0.7 constant_dynamic-update-slice_fusion.2
  2.2 0.7 constant_dynamic-update-slice_fusion.1
  2.9 0.7 constant_dynamic-update-slice_fusion
  3.6 2.2 %all-gather = bf16[256,258]{0,1:T(8,128)(2,1)S(1)} all-gather(bf16[128,258]{0,1:T(8,128)(2,1)S(1)} %constant_dynamic-update-slice_fusion), channel_id=2, replica_groups=mesh['groups'=2,'rows'=4,'keys'=2,'heads'=2] {'heads'}, dimensions={0}, use_global_device_ids=true | all-gather | bytes 198144 | tf_op jit(solution)/shard_map/all_gather | solution.py:378
  5.8 0.1 reshape.22
  6.0 0.6 pad.4.w_ref
  6.6 9.1 %pair_bias.1 = bf16[4,128,128]{2,1,0:T(8,128)(2,1)} custom-call(s32[1]{0:T(128)} %bitcast._, bf16[128,256,128]{2,1,0:T(8,128)(2,1)} %pair_ref.3, f32[1,128]{1,0:T(1,128)} %bitcast.40, bf16[16,128]{1,0:T(8,128)(2,1)} %pad.4.w_ref), custom_call_target="tpu_custom_call" | custom-call | flops 419430400 | bytes 4194304 | tf_op jit(solution)/shard_map/pair_bias/pallas_call | solution.py:54
  15.6 1.2 collective-permute-start
  16.9 1.4 constant_dynamic-slice_fusion
  18.3 0.3 collective-permute-start.7
  18.6 0.1 slice.33
  18.7 0.1 constant_dynamic-slice_fusion.5
  18.8 0.6 pad_add_fusion.info_ref
  19.4 0.7 copy.31.counts_ref
  20.1 0.1 copy.25
  20.3 0.1 copy.26
  20.4 0.1 copy.27
  20.5 0.1 copy.28
  21.3 0.7 pad_maximum_fusion.4.w_ref
  22.0 0.9 pad_maximum_fusion.3
  22.9 3.2 %collective-permute-start.1 = (bf16[2,4,128,128]{3,2,1,0:T(8,128)(2,1)S(1)}, bf16[2,4,128,128]{3,2,1,0:T(8,128)(2,1)S(1)}, u32[]{:S(2)}, u32[]{:S(2)}) collective-permute-start(bf16[2,4,128,128]{3,2,1,0:T(8,128)(2,1)S(1)} %pad_maximum_fusion.3), channel_id=1, source_target_pairs={{0,4},{4,8},{10,14},{14,2},{1,5},{5,9},{11,15},{15,3},{16,20},{20,... | collective-permute-start | bytes 786440 | tf_op jit(solution)/shard_map/ppermute | solution.py:340
  26.1 1.7 collective-permute-start.2
  27.8 2.9 %collective-permute-start.3 = (bf16[2,4,128,128]{3,2,1,0:T(8,128)(2,1)S(1)}, bf16[2,4,128,128]{3,2,1,0:T(8,128)(2,1)S(1)}, u32[]{:S(2)}, u32[]{:S(2)}) collective-permute-start(bf16[2,4,128,128]{3,2,1,0:T(8,128)(2,1)S(1)} %pad_maximum_fusion.3), channel_id=1, source_target_pairs={{0,12},{4,0},{10,6},{14,10},{1,13},{5,1},{11,7},{15,11},{16,28},{2... | collective-permute-start | bytes 786440 | tf_op jit(solution)/shard_map/ppermute | solution.py:340
  30.7 29.8 %own_rows.1 = (bf16[64,256,256]{2,1,0:T(8,128)(2,1)}, bf16[64,256,128]{2,1,0:T(8,128)(2,1)}, f32[64,256,128]{2,1,0:T(8,128)}) custom-call(s32[3]{0:T(128)} %pad_add_fusion.info_ref, s32[1]{0:T(128)S(6)} %copy.41.seq_ref, s32[64,4]{1,0:T(8,128)} %copy.31.counts_ref, bf16[128,256,128]{2,1,0:T(8,128)(2,1)} %pair_ref.3, f32[1,128]{1,0:T(1,128)} %bitcast.41, ...), custom_call_target="tpu_custom_call" | custom-call | flops 16777216000 | bytes 25165824 | tf_op jit(solution)/shard_map/own_rows/pallas_call | solution.py:112
  60.5 0.0 collective-permute-done.1
  60.5 0.0 collective-permute-done.2
  60.5 0.1 pad_maximum_fusion
  60.7 0.9 pad_maximum_fusion.2
  61.6 1.5 collective-permute-start.5
  63.1 1.5 constant_dynamic-slice_fusion.1
  64.6 0.1 collective-permute-start.6
  64.7 2.6 %constant_dynamic-slice_fusion.4 = bf16[20,256,128]{2,1,0:T(8,128)(2,1)} fusion(bf16[128,256,128]{2,1,0:T(8,128)(2,1)} %pair_ref.3, s32[]{:T(128)S(6)} %select_n.34), kind=kLoop, calls=%fused_computation.24 | loop fusion | bytes 2621444 | tf_op jit(solution)/shard_map/dynamic_slice | solution.py:394
  67.3 1.4 collective-permute-start.4
  68.7 0.6 pad_maximum_fusion.5.refs_5_
  69.3 1.4 fusion.1
  70.8 1.1 pad_maximum_fusion.1.refs_7_
  71.9 32.3 %row_attention.3 = (bf16[128,128,128]{2,1,0:T(8,128)(2,1)}, bf16[1,20,128,128]{3,2,1,0:T(8,128)(2,1)}) custom-call(s32[3]{0:T(128)} %pad_add_fusion.info_ref, s32[1]{0:T(128)S(6)} %copy.41.seq_ref, s32[64,4]{1,0:T(8,128)} %copy.31.counts_ref, bf16[64,256,256]{2,1,0:T(8,128)(2,1)} %get-tuple-element.25.refs_0_, ...), custom_call_target="tpu_custom_call" | custom-call | flops 10737418240 | bytes 5242880 | tf_op jit(solution)/shard_map/row_attention/pallas_call | solution.py:273
  104.1 1.6 collective-permute-start.8
  105.7 37.7 %row_attention.4 = (bf16[128,128,128]{2,1,0:T(8,128)(2,1)}, bf16[1,24,128,128]{3,2,1,0:T(8,128)(2,1)}) custom-call(s32[3]{0:T(128)} %pad_add_fusion.info_ref, s32[1]{0:T(128)S(6)} %copy.41.seq_ref, s32[64,4]{1,0:T(8,128)} %copy.31.counts_ref, bf16[64,256,256]{2,1,0:T(8,128)(2,1)} %get-tuple-element.25.refs_0_, ...), custom_call_target="tpu_custom_call", output_to_operand_aliasing={{0}: (11, {})} | custom-call | flops 12884901888 | bytes 6291456 | tf_op jit(solution)/shard_map/row_attention/pallas_call | solution.py:273
  143.5 2.0 %collective-permute-start.9 = (bf16[24,128,128]{2,1,0:T(8,128)(2,1)}, bf16[24,128,128]{2,1,0:T(8,128)(2,1)S(1)}, u32[]{:S(2)}, u32[]{:S(2)}) collective-permute-start(bf16[24,128,128]{2,1,0:T(8,128)(2,1)} %bitcast.45), channel_id=1, source_target_pairs={{0,1},{1,0},{2,3},{3,2},{4,5},{5,4},{6,7},{7,6},{8,9},{9,8},{10,11... | collective-permute-start | bytes 2359304 | tf_op jit(solution)/shard_map/ppermute | solution.py:322
  145.5 31.9 %row_attention.5 = (bf16[128,128,128]{2,1,0:T(8,128)(2,1)}, bf16[1,20,128,128]{3,2,1,0:T(8,128)(2,1)}) custom-call(s32[3]{0:T(128)} %pad_add_fusion.info_ref, s32[1]{0:T(128)S(6)} %copy.41.seq_ref, s32[64,4]{1,0:T(8,128)} %copy.31.counts_ref, bf16[64,256,256]{2,1,0:T(8,128)(2,1)} %get-tuple-element.25.refs_0_, ...), custom_call_target="tpu_custom_call", output_to_operand_aliasing={{0}: (11, {})} | custom-call | flops 10737418240 | bytes 5242880 | tf_op jit(solution)/shard_map/row_attention/pallas_call | solution.py:273
  177.4 1.0 collective-permute-start.10
  178.4 0.9 constant_dynamic-update-slice_fusion.7
  179.3 0.9 constant_dynamic-update-slice_fusion.6
  180.3 0.1 collective-permute-done.10
  180.4 0.9 constant_dynamic-update-slice_fusion.5
  (15 shorter events, 0.1 us)
Async XLA Ops:
  0.0 18.7 %copy-start = (s32[128,4]{0,1:T(4,128)S(1)}, s32[128,4]{0,1:T(4,128)}, u32[]{:S(2)}) copy-start(s32[128,4]{0,1:T(4,128)} %param.12) | copy-start | bytes 6148
  15.6 6.3 %collective-permute-start = (bf16[4,128,128]{2,1,0:T(8,128)(2,1)}, bf16[4,128,128]{2,1,0:T(8,128)(2,1)S(1)}, u32[]{:S(2)}, u32[]{:S(2)}) collective-permute-start(bf16[4,128,128]{2,1,0:T(8,128)(2,1)} %pair_bias.1), channel_id=1, source_target_pairs={{0,2},{2,0},{1,3},{3,1},{4,6},{6,4},{5,7},{7,5},{8,10},{10,8},{9,1... | collective-permute-start | bytes 393224 | tf_op jit(solution)/shard_map/ppermute | solution.py:322
  18.3 53.6 %collective-permute-start.7 = (bf16[20,256,128]{2,1,0:T(8,128)(2,1)S(1)}, bf16[20,256,128]{2,1,0:T(8,128)(2,1)}, u32[]{:S(2)}, u32[]{:S(2)}) collective-permute-start(bf16[20,256,128]{2,1,0:T(8,128)(2,1)S(1)} %constant_dynamic-slice_fusion), channel_id=1, source_target_pairs={{0,2},{2,0},{1,3},{3,1},{4,6},{6,4},{5,7},{7,5},{8,10},{10,8},{9,1... | collective-permute-start | bytes 3932168 | tf_op jit(solution)/shard_map/ppermute | solution.py:322
  22.9 37.6 %collective-permute-start.1 = (bf16[2,4,128,128]{3,2,1,0:T(8,128)(2,1)S(1)}, bf16[2,4,128,128]{3,2,1,0:T(8,128)(2,1)S(1)}, u32[]{:S(2)}, u32[]{:S(2)}) collective-permute-start(bf16[2,4,128,128]{3,2,1,0:T(8,128)(2,1)S(1)} %pad_maximum_fusion.3), channel_id=1, source_target_pairs={{0,4},{4,8},{10,14},{14,2},{1,5},{5,9},{11,15},{15,3},{16,20},{20,... | collective-permute-start | bytes 786440 | tf_op jit(solution)/shard_map/ppermute | solution.py:340
  26.1 34.4 %collective-permute-start.2 = (bf16[2,4,128,128]{3,2,1,0:T(8,128)(2,1)S(1)}, bf16[2,4,128,128]{3,2,1,0:T(8,128)(2,1)S(1)}, u32[]{:S(2)}, u32[]{:S(2)}) collective-permute-start(bf16[2,4,128,128]{3,2,1,0:T(8,128)(2,1)S(1)} %pad_maximum_fusion.3), channel_id=1, source_target_pairs={{0,8},{4,12},{10,2},{14,6},{1,9},{5,13},{11,3},{15,7},{16,24},{20,... | collective-permute-start | bytes 786440 | tf_op jit(solution)/shard_map/ppermute | solution.py:340
  27.8 32.7 %collective-permute-start.3 = (bf16[2,4,128,128]{3,2,1,0:T(8,128)(2,1)S(1)}, bf16[2,4,128,128]{3,2,1,0:T(8,128)(2,1)S(1)}, u32[]{:S(2)}, u32[]{:S(2)}) collective-permute-start(bf16[2,4,128,128]{3,2,1,0:T(8,128)(2,1)S(1)} %pad_maximum_fusion.3), channel_id=1, source_target_pairs={{0,12},{4,0},{10,6},{14,10},{1,13},{5,1},{11,7},{15,11},{16,28},{2... | collective-permute-start | bytes 786440 | tf_op jit(solution)/shard_map/ppermute | solution.py:340
  61.6 7.7 %collective-permute-start.5 = (bf16[2,2,4,128,128]{4,3,2,1,0:T(8,128)(2,1)}, bf16[2,2,4,128,128]{4,3,2,1,0:T(8,128)(2,1)}, u32[]{:S(2)}, u32[]{:S(2)}) collective-permute-start(bf16[2,2,4,128,128]{4,3,2,1,0:T(8,128)(2,1)} %get-tuple-element.43), channel_id=1, source_target_pairs={{0,1},{1,0},{2,3},{3,2},{4,5},{5,4},{6,7},{7,6},{8,9},{9,8},{10,11... | collective-permute-start | bytes 1572872 | tf_op jit(solution)/shard_map/ppermute | solution.py:322
  64.6 41.1 %collective-permute-start.6 = (bf16[24,256,128]{2,1,0:T(8,128)(2,1)S(1)}, bf16[24,256,128]{2,1,0:T(8,128)(2,1)}, u32[]{:S(2)}, u32[]{:S(2)}) collective-permute-start(bf16[24,256,128]{2,1,0:T(8,128)(2,1)S(1)} %constant_dynamic-slice_fusion.1), channel_id=1, source_target_pairs={{0,2},{2,0},{1,3},{3,1},{4,6},{6,4},{5,7},{7,5},{8,10},{10,8},{9,1... | collective-permute-start | bytes 4718600 | tf_op jit(solution)/shard_map/ppermute | solution.py:322
  67.3 78.2 %collective-permute-start.4 = (bf16[20,256,128]{2,1,0:T(8,128)(2,1)}, bf16[20,256,128]{2,1,0:T(8,128)(2,1)}, u32[]{:S(2)}, u32[]{:S(2)}) collective-permute-start(bf16[20,256,128]{2,1,0:T(8,128)(2,1)} %constant_dynamic-slice_fusion.4), channel_id=1, source_target_pairs={{0,2},{2,0},{1,3},{3,1},{4,6},{6,4},{5,7},{7,5},{8,10},{10,8},{9,1... | collective-permute-start | bytes 3932168 | tf_op jit(solution)/shard_map/ppermute | solution.py:322
  104.1 74.3 %collective-permute-start.8 = (bf16[20,128,128]{2,1,0:T(8,128)(2,1)}, bf16[20,128,128]{2,1,0:T(8,128)(2,1)S(1)}, u32[]{:S(2)}, u32[]{:S(2)}) collective-permute-start(bf16[20,128,128]{2,1,0:T(8,128)(2,1)} %bitcast.46), channel_id=1, source_target_pairs={{0,1},{1,0},{2,3},{3,2},{4,5},{5,4},{6,7},{7,6},{8,9},{9,8},{10,11... | collective-permute-start | bytes 1966088 | tf_op jit(solution)/shard_map/ppermute | solution.py:322
  143.5 35.9 %collective-permute-start.9 = (bf16[24,128,128]{2,1,0:T(8,128)(2,1)}, bf16[24,128,128]{2,1,0:T(8,128)(2,1)S(1)}, u32[]{:S(2)}, u32[]{:S(2)}) collective-permute-start(bf16[24,128,128]{2,1,0:T(8,128)(2,1)} %bitcast.45), channel_id=1, source_target_pairs={{0,1},{1,0},{2,3},{3,2},{4,5},{5,4},{6,7},{7,6},{8,9},{9,8},{10,11... | collective-permute-start | bytes 2359304 | tf_op jit(solution)/shard_map/ppermute | solution.py:322
  177.4 2.9 %collective-permute-start.10 = (bf16[20,128,128]{2,1,0:T(8,128)(2,1)}, bf16[20,128,128]{2,1,0:T(8,128)(2,1)S(1)}, u32[]{:S(2)}, u32[]{:S(2)}) collective-permute-start(bf16[20,128,128]{2,1,0:T(8,128)(2,1)} %bitcast.47), channel_id=1, source_target_pairs={{0,1},{1,0},{2,3},{3,2},{4,5},{5,4},{6,7},{7,6},{8,9},{9,8},{10,11... | collective-permute-start | bytes 1966088 | tf_op jit(solution)/shard_map/ppermute | solution.py:322
